TPU v7x, 32 devices: a whole 2x2x4 slice. The times are simulated.
32 devices in a mesh: fluid: 8 (over z, y), grp: 4 (over x, core).
Axes of the slice: x: 2, y: 2, z: 4, core: 2. Of those that a mesh axis runs over, the one named last changes fastest.
Arguments:
- acoustic_modes: bfloat16 [262144, 400], P(('fluid', 'grp')), may hold values from -6 to 6
- shell_modes: bfloat16 [8192, 300], P('fluid'), may hold values from -0.0012207031 to 0.0012207031
- wet_counts: int32 [32], P(('fluid', 'grp')), may hold values from 1 to 2048, 26214 in all
- fluid_nodes: int32 [65536], P(('fluid', 'grp')), may hold values from 0 to 8191
- shell_nodes: int32 [65536], P(('fluid', 'grp')), may hold values from 0 to 1023
- wet_area: float32 [65536], P(('fluid', 'grp')), may hold values from 0.15 to 0.6
- shell_freq: float32 [300], replicated, may hold values from 1 to 2
- shell_loss: float32 [300], replicated, may hold values from 0.2 to 0.5
- cavity_freq: float32 [400], replicated, may hold values from 1 to 2
- cavity_loss: float32 [400], replicated, may hold values from 0.2 to 0.5
- freqs: float32 [64], replicated, may hold values from 0.7 to 2.2
- modal_force: float32 [300], replicated, may hold values from -1.5 to 1.5
- cavity_source: float32 [400], replicated, may hold values from -1.5 to 1.5
Outputs:
- pressure: bfloat16 [262144, 128], P(('fluid', 'grp'))
- modal_structure: float32 [2, 64, 300], P(None, 'grp')
Inputs may be any that keep to these rules, and one draw needn't show every extreme that they name: `wet_counts`: slots 0 to count - 1 of a device's 2048 interface slots are live, the others are ignored. `fluid_nodes`: numbered within the device's own 8192 cavity rows. `shell_nodes`: numbered within the 1024 shell rows of the device's fluid index.
All inputs are finite; a program needn't handle non-finite values.
Results may differ from a plain program's by a relative error of at most 0.0055.
Values may be sent and summed in bfloat16 or wider, within the bound.
No kernel may reach another device: no remote copies, remote signals or barrier semaphores. Data moves between devices by JAX's collectives and lax.ppermute only.
A program may use at most 64 MiB of HBM per device.

v0:
```python
import math
import jax
import jax.numpy as jnp
from jax import lax
from jax.sharding import PartitionSpec as P

SECTIONS = 4
HIGH = lax.Precision.HIGHEST


def divide_complex(real_part, imag_part, denom_real, denom_imag):
    scale = denom_real * denom_real + denom_imag * denom_imag
    return (
        (real_part * denom_real + imag_part * denom_imag) / scale,
        (imag_part * denom_real - real_part * denom_imag) / scale,
    )


def modal_terms(omega, loss, freqs):
    stiff = omega * omega
    real_part = stiff[None, :] - (freqs * freqs)[:, None]
    imag_part = jnp.broadcast_to((loss * stiff)[None, :], real_part.shape)
    return (real_part, imag_part)


def couple_rows(shell_modes, wet_rows, node_rows, live_counts):
    depth, width, cavity = wet_rows.shape
    block = math.gcd(depth, 256)
    result = jnp.zeros((shell_modes.shape[1], cavity), jnp.float32)
    source = 0

    def add_block(number, carry, source=source):
        first = number * block
        piece = lax.dynamic_slice(wet_rows, (first, source, 0), (block, 1, cavity)).reshape(
            block, cavity
        )
        picks = lax.dynamic_slice(node_rows, (first, source), (block, 1)).reshape(block)
        shell_rows = shell_modes[picks]
        return carry + lax.dot_general(
            shell_rows, piece, (((0,), (0,)), ((), ())), preferred_element_type=jnp.float32
        )

    result = lax.fori_loop(0, (live_counts[source] + block - 1) // block, add_block, result)
    return result


def on_device(
    acoustic_modes,
    shell_modes,
    wet_counts,
    fluid_nodes,
    shell_nodes,
    wet_area,
    shell_freq,
    shell_loss,
    cavity_freq,
    cavity_loss,
    freqs,
    modal_force,
    cavity_source,
):
    groups = lax.axis_size("grp")
    member = lax.axis_index("grp")
    slots = fluid_nodes.shape[0]
    freq_total = freqs.shape[0]
    freq_count = freq_total // groups
    count = wet_counts[0]
    live = (jnp.arange(slots, dtype=jnp.int32) < count).astype(jnp.float32)
    wet_rows = (
        wet_area[:, None] * acoustic_modes[fluid_nodes].astype(jnp.float32) * live[:, None]
    ).astype(jnp.bfloat16)
    partial_sum = couple_rows(shell_modes, wet_rows[:, None, :], shell_nodes[:, None], [count])
    ds_re, ds_im = modal_terms(shell_freq, shell_loss, freqs)
    da_re, da_im = modal_terms(cavity_freq, cavity_loss, freqs)
    free_re, free_im = divide_complex(
        jnp.broadcast_to(cavity_source[None, :], da_re.shape), jnp.zeros_like(da_re), da_re, da_im
    )
    free_amps = jnp.concatenate([free_re, free_im], 0).astype(jnp.bfloat16)
    free_field = lax.dot_general(
        acoustic_modes, free_amps, (((1,), (1,)), ((), ())), preferred_element_type=jnp.float32
    )
    squared = (freqs * freqs)[:, None]
    coupling = lax.psum(partial_sum, ("fluid", "grp"))
    start = member * freq_count

    def own_rows(values):
        return lax.dynamic_slice_in_dim(values, start, freq_count, 0)

    shell_re, shell_im = (own_rows(ds_re), own_rows(ds_im))
    cavity_re, cavity_im = (own_rows(da_re), own_rows(da_im))
    base_re, base_im = (own_rows(free_re), own_rows(free_im))
    own_squared = own_rows(squared)
    coupled_re = jnp.zeros_like(base_re)
    coupled_im = jnp.zeros_like(base_im)
    for section in range(SECTIONS):
        amounts = jnp.concatenate([base_re + coupled_re, base_im + coupled_im], 0)
        loads = jnp.dot(amounts, coupling.T, precision=HIGH)
        struct_re, struct_im = divide_complex(
            modal_force[None, :] + loads[:freq_count], loads[freq_count:], shell_re, shell_im
        )
        back = jnp.dot(jnp.concatenate([struct_re, struct_im], 0), coupling, precision=HIGH)
        coupled_re, coupled_im = divide_complex(
            own_squared * back[:freq_count], own_squared * back[freq_count:], cavity_re, cavity_im
        )
    mine = jnp.stack([coupled_re, coupled_im]).astype(jnp.bfloat16)
    coupled_amps = lax.all_gather(mine, "grp", axis=1, tiled=True).reshape(2 * freq_total, -1)
    modal_structure = jnp.stack([struct_re, struct_im])
    coupled_field = lax.dot_general(
        acoustic_modes, coupled_amps, (((1,), (1,)), ((), ())), preferred_element_type=jnp.float32
    )
    pressure = (free_field + coupled_field).astype(jnp.bfloat16)
    return (pressure, modal_structure)


def solution(mesh):
    placed = (
        P(("fluid", "grp"), None),
        P("fluid", None),
        P(("fluid", "grp")),
        P(("fluid", "grp")),
        P(("fluid", "grp")),
        P(("fluid", "grp")),
        P(),
        P(),
        P(),
        P(),
        P(),
        P(),
        P(),
    )
    return jax.shard_map(
        on_device,
        mesh=mesh,
        in_specs=placed,
        out_specs=(P(("fluid", "grp"), None), P(None, "grp", None)),
        check_vma=False,
    )
```

profile of v0, /device:TPU:9, one launch (start us, length us, event | category | flops | bytes accessed | tf_op | source)
XLA Modules:
  0.0 214.8 jit_solution(2672962643485708296)
XLA Ops:
  7.9 10.7 %copy.19 = bf16[8192,400]{1,0:T(8,128)(2,1)} copy(bf16[8192,400]{0,1:T(8,128)(2,1)} %param.15) | data formatting | bytes 13107200 | tf_op args[0]
  18.6 12.1 %gather_fusion.1 = bf16[2048,400]{1,0:T(8,128)(2,1)S(1)} fusion(bf16[8192,400]{1,0:T(8,128)(2,1)} %copy.19, s32[2048]{0:T(1024)S(1)} %fusion.69), kind=kCustom, calls=%fused_computation.1 | custom fusion | bytes 3284992 | tf_op jit(solution)/shard_map/gather | solution.py:70
  30.7 1.7 fusion.6
  32.4 2.8 %copy.21 = bf16[2048,1,400]{0,2,1:T(8,128)(2,1)S(1)} copy(bf16[2048,1,400]{2,0,1:T(8,128)(2,1)} %fusion.6) | data formatting | bytes 3276800 | tf_op jit(solution)/shard_map/while | solution.py:43
  35.2 1.4 copy.20
  36.7 17.5 %while.10 = (s32[]{:T(128)}, f32[300,400]{0,1:T(8,128)S(1)}, s32[]{:T(128)}, s32[2048,1]{0,1:T(1,128)}, bf16[1024,300]{1,0:T(8,128)(2,1)S(1)}, /*index=5*/bf16[2...) while((s32[]{:T(128)}, f32[300,400]{0,1:T(8,128)S(1)}, s32[]{:T(128)}, ...), condition=%wide.region_1.2_spmd, body=%wide.region_0.1_spmd.sunk | while | flops 61561796 | bytes 1811355 | solution.py:43
  36.8 0.7 compare_select_fusion.3
  37.5 1.2 gather_fusion
  39.0 0.7 compare_select_fusion.3
  39.7 1.2 gather_fusion
  41.2 0.7 compare_select_fusion.3
  41.8 1.2 gather_fusion
  43.3 0.7 compare_select_fusion.3
  44.0 1.2 gather_fusion
  45.5 0.7 compare_select_fusion.3
  46.2 1.2 gather_fusion
  47.7 0.7 compare_select_fusion.3
  48.4 1.2 gather_fusion
  50.6 1.2 gather_fusion
  52.1 0.7 compare_select_fusion.3
  52.8 1.2 gather_fusion
  54.3 0.8 copy-done.1
  55.4 6.2 %fusion.12 = f32[128,8192]{1,0:T(8,128)} fusion(bf16[8192,400]{0,1:T(8,128)(2,1)} %param.15, bf16[64,400]{1,0:T(8,128)(2,1)S(1)} %get-tuple-element.88, bf16[64,400]{1,0:T(8,128)(2,1)S(1)} %get-tuple-element.85), kind=kOutput, calls=%fused_computation.22 | convolution fusion | flops 839065600 | bytes 10850304 | tf_op jit(solution)/shard_map/dot_general | solution.py:79
  61.6 120.4 %all-reduce.2.cloned.1.call-done = f32[300,400]{0,1:T(8,128)} async-done(((f32[300,400]{0,1:T(8,128)}), f32[300,400]{0,1:T(8,128)}) %all-reduce.2.cloned.1.call-update) | async-done | bytes 480016 | tf_op jit(solution)/shard_map/psum | solution.py:83
  182.1 1.7 fusion.16
  183.8 1.8 fusion.32
  185.7 1.5 fusion.20
  187.3 1.8 fusion.36
  189.1 1.5 fusion.24
  192.8 7.9 %all_gather.3 = bf16[2,64,400]{2,1,0:T(8,128)(2,1)S(1)} all-gather(bf16[2,16,400]{2,1,0:T(8,128)(2,1)S(1)} %pad_maximum_fusion.1), channel_id=1, replica_groups=mesh['fluid'=8,'grp'=4] {'grp'}, dimensions={1}, use_global_device_ids=true | all-gather | bytes 128000 | tf_op jit(solution)/shard_map/all_gather | solution.py:106
  200.7 4.1 %fusion.4 = bf16[8192,128]{0,1:T(8,128)(2,1)S(1)} fusion(f32[128,8192]{1,0:T(8,128)S(1)} %copy-done.2, bf16[128,400]{1,0:T(8,128)(2,1)S(1)} %bitcast.38, bf16[8192,400]{0,1:T(8,128)(2,1)} %param.15), kind=kOutput, calls=%fused_computation.10 | convolution fusion | flops 840957952 | bytes 12947456 | tf_op jit(solution)/shard_map/dot_general | solution.py:108
  204.9 2.4 %copy.22 = bf16[8192,128]{1,0:T(8,128)(2,1)} copy(bf16[8192,128]{0,1:T(8,128)(2,1)S(1)} %fusion.4) | data formatting | bytes 4194304
  (65 shorter events, 6.7 us)
Async XLA Ops:
  7.2 174.9 %all-reduce.2.cloned.1.call-start = ((), (), s32[]{:S(2)}) async-start(), calls=%async_computation | async-start | bytes 1228800 | tf_op jit(solution)/shard_map/psum | solution.py:83
  7.9 10.7 %copy-start.6 = (s32[2048]{0:T(1024)S(1)}, s32[2048]{0:T(1024)}, u32[]{:S(2)}) copy-start(s32[2048]{0:T(1024)} %param.18) | copy-start | bytes 24580
  18.6 12.1 %copy-start.4 = (f32[2048]{0:T(1024)S(1)}, f32[2048]{0:T(1024)}, u32[]{:S(2)}) copy-start(f32[2048]{0:T(1024)} %param.20) | copy-start | bytes 24580
  36.7 18.4 %copy-start.11 = (f32[64]{0:T(128)S(1)}, f32[64]{0:T(128)}, u32[]{:S(2)}) copy-start(f32[64]{0:T(128)} %param.25) | copy-start | bytes 772
  36.7 18.5 %copy-start.7 = (f32[400]{0:T(512)S(1)}, f32[400]{0:T(512)}, u32[]{:S(2)}) copy-start(f32[400]{0:T(512)} %param.24) | copy-start | bytes 4804
  36.7 18.5 %copy-start.8 = (f32[400]{0:T(512)S(1)}, f32[400]{0:T(512)}, u32[]{:S(2)}) copy-start(f32[400]{0:T(512)} %param.23) | copy-start | bytes 4804
  36.7 18.5 %copy-start.5 = (f32[400]{0:T(512)S(1)}, f32[400]{0:T(512)}, u32[]{:S(2)}) copy-start(f32[400]{0:T(512)} %param.27) | copy-start | bytes 4804
  54.3 0.8 copy-start.1
  55.3 6.3 %copy-start.9 = (f32[300]{0:T(512)S(1)}, f32[300]{0:T(512)}, u32[]{:S(2)}) copy-start(f32[300]{0:T(512)} %param.22) | copy-start | bytes 3604
  55.4 6.3 %copy-start.10 = (f32[300]{0:T(512)S(1)}, f32[300]{0:T(512)}, u32[]{:S(2)}) copy-start(f32[300]{0:T(512)} %param.21) | copy-start | bytes 3604
  55.4 128.3 %copy-start.3 = (f32[300]{0:T(512)S(1)}, f32[300]{0:T(512)}, u32[]{:S(2)}) copy-start(f32[300]{0:T(512)} %param.26) | copy-start | bytes 3604
  182.0 8.7 %copy-start = (f32[300,400]{0,1:T(8,128)S(1)}, f32[300,400]{0,1:T(8,128)}, u32[]{:S(2)}) copy-start(f32[300,400]{0,1:T(8,128)} %all-reduce.2.cloned.1.call-done) | copy-start | bytes 1440004
  182.1 18.7 %copy-start.2 = (f32[128,8192]{1,0:T(8,128)S(1)}, f32[128,8192]{1,0:T(8,128)}, u32[]{:S(2)}) copy-start(f32[128,8192]{1,0:T(8,128)} %fusion.12) | copy-start | bytes 12582916
Sparse Core Ops, SparseCore 0:
  55.2 126.7 all-reduce.1
where the time goes:
time: 216 us; the launch traced here: 215 us
  waiting for transfers between devices  120 us (56%)
  local copies, waits for them, and re-layouts  39.7 us (18%)
  matrix products  22.6 us (10%)
  between operations  15 us (7%)
  other arithmetic  8.73 us (4%)
  blocking collectives  7.9 us (4%)
    psum x1, waiting for transfers between devices, on_device(): coupling = lax.psum(partial_sum, ('fluid', 'grp'))  120 us
    unnamed x26, local copies, waits for them, and re-layouts  14 us
    gather x1, local copies, waits for them, and re-layouts, on_device(): acoustic_modes[fluid_nodes].astype(jnp.float32)  12.1 us
    gather x8, local copies, waits for them, and re-layouts, add_block(): shell_rows = shell_modes[picks]  9.31 us
    all_gather x1, blocking collectives, on_device(): lax.all_gather(mine, 'grp', axis=1, tiled=True).reshape(2 * freq_total, -1)  7.9 us
    dot_general x1, matrix products, on_device(): lax.dot_general(acoustic_modes, free_amps, (((1,), (1,)), ((), ())), pref...  6.15 us
    select_n x8, other arithmetic, add_block(): shell_rows = shell_modes[picks]  5.49 us
    dot_general x4, matrix products, on_device(): loads = jnp.dot(amounts, coupling.T, precision=HIGH)  5.1 us
  transfers between devices with their start and end apart: 1, of which 1 were waited for; matrix products, arithmetic and copies ran while one was open for 3% of the time, Pallas kernels for 0%

commit v1 on v0

--- a/solution.py
+++ b/solution.py
@@ -80,7 +80,7 @@
         acoustic_modes, free_amps, (((1,), (1,)), ((), ())), preferred_element_type=jnp.float32
     )
     squared = (freqs * freqs)[:, None]
-    coupling = lax.psum(partial_sum, ("fluid", "grp"))
+    coupling = lax.psum(lax.psum(partial_sum, "grp"), "fluid")
     start = member * freq_count
 
     def own_rows(values):

time: 216 us -> 198 us (0.917)
  waiting for transfers between devices: 120 us -> 102 us
    psum x1 -> x2, waiting for transfers between devices: 120 us -> 102 us  [on_device(): coupling = lax.psum(lax.psum(partial_sum, 'grp'), 'fluid')]
  transfers between devices with their start and end apart: 1 -> 2, of which waited for: 1 -> 2; matrix products, arithmetic and copies ran while one was open for 3% -> 3% of each run, Pallas kernels for 0% -> 0%
where the time goes in v1:
time: 198 us; the launch traced here: 196 us
  waiting for transfers between devices  102 us (52%)
  local copies, waits for them, and re-layouts  39.8 us (20%)
  matrix products  22.5 us (11%)
  between operations  15.1 us (8%)
  other arithmetic  8.73 us (4%)
  blocking collectives  7.42 us (4%)
    psum x2, waiting for transfers between devices, on_device(): coupling = lax.psum(lax.psum(partial_sum, 'grp'), 'fluid')  102 us
    unnamed x26, local copies, waits for them, and re-layouts  14 us
    gather x1, local copies, waits for them, and re-layouts, on_device(): acoustic_modes[fluid_nodes].astype(jnp.float32)  12.1 us
    gather x8, local copies, waits for them, and re-layouts, add_block(): shell_rows = shell_modes[picks]  9.31 us
    all_gather x1, blocking collectives, on_device(): lax.all_gather(mine, 'grp', axis=1, tiled=True).reshape(2 * freq_total, -1)  7.42 us
    dot_general x1, matrix products, on_device(): lax.dot_general(acoustic_modes, free_amps, (((1,), (1,)), ((), ())), pref...  6.06 us
    select_n x8, other arithmetic, add_block(): shell_rows = shell_modes[picks]  5.49 us
    dot_general x4, matrix products, on_device(): loads = jnp.dot(amounts, coupling.T, precision=HIGH)  5.1 us
  transfers between devices with their start and end apart: 2, of which 2 were waited for; matrix products, arithmetic and copies ran while one was open for 3% of the time, Pallas kernels for 0%

profile of v1, /device:TPU:9, one launch (start us, length us, event | category | flops | bytes accessed | tf_op | source)
XLA Modules:
  0.0 196.0 jit_solution(5997298084784146419)
XLA Ops:
  7.9 10.7 %copy.19 = bf16[8192,400]{1,0:T(8,128)(2,1)} copy(bf16[8192,400]{0,1:T(8,128)(2,1)} %param.15) | data formatting | bytes 13107200 | tf_op args[0]
  18.6 12.1 %gather_fusion.1 = bf16[2048,400]{1,0:T(8,128)(2,1)S(1)} fusion(bf16[8192,400]{1,0:T(8,128)(2,1)} %copy.19, s32[2048]{0:T(1024)S(1)} %fusion.69), kind=kCustom, calls=%fused_computation.1 | custom fusion | bytes 3284992 | tf_op jit(solution)/shard_map/gather | solution.py:70
  30.7 1.7 fusion.6
  32.4 2.8 %copy.21 = bf16[2048,1,400]{0,2,1:T(8,128)(2,1)S(1)} copy(bf16[2048,1,400]{2,0,1:T(8,128)(2,1)} %fusion.6) | data formatting | bytes 3276800 | tf_op jit(solution)/shard_map/while | solution.py:43
  35.2 1.4 copy.20
  36.8 17.5 %while.10 = (s32[]{:T(128)}, f32[300,400]{0,1:T(8,128)S(1)}, s32[]{:T(128)}, s32[2048,1]{0,1:T(1,128)}, bf16[1024,300]{1,0:T(8,128)(2,1)S(1)}, /*index=5*/bf16[2...) while((s32[]{:T(128)}, f32[300,400]{0,1:T(8,128)S(1)}, s32[]{:T(128)}, ...), condition=%wide.region_1.2_spmd, body=%wide.region_0.1_spmd.sunk | while | flops 61561796 | bytes 1811355 | solution.py:43
  36.8 0.7 compare_select_fusion.3
  37.5 1.2 gather_fusion
  39.0 0.7 compare_select_fusion.3
  39.7 1.2 gather_fusion
  41.2 0.7 compare_select_fusion.3
  41.9 1.2 gather_fusion
  43.4 0.7 compare_select_fusion.3
  44.1 1.2 gather_fusion
  45.6 0.7 compare_select_fusion.3
  46.2 1.2 gather_fusion
  47.7 0.7 compare_select_fusion.3
  48.4 1.2 gather_fusion
  50.6 1.2 gather_fusion
  52.8 1.2 gather_fusion
  54.3 0.8 copy-done.1
  55.5 32.0 %all-reduce.3.cloned.1.call-done = f32[300,400]{0,1:T(8,128)} async-done(((f32[300,400]{0,1:T(8,128)}), f32[300,400]{0,1:T(8,128)}) %all-reduce.3.cloned.1.call-update) | async-done | bytes 480016 | tf_op jit(solution)/shard_map/psum | solution.py:83
  87.6 6.1 %fusion.12 = f32[128,8192]{1,0:T(8,128)} fusion(bf16[8192,400]{0,1:T(8,128)(2,1)} %param.15, bf16[64,400]{1,0:T(8,128)(2,1)S(1)} %get-tuple-element.88, bf16[64,400]{1,0:T(8,128)(2,1)S(1)} %get-tuple-element.85), kind=kOutput, calls=%fused_computation.22 | convolution fusion | flops 839065600 | bytes 10850304 | tf_op jit(solution)/shard_map/dot_general | solution.py:79
  93.6 70.1 %all-reduce.5.cloned.1.call-done = f32[300,400]{0,1:T(8,128)} async-done(((f32[300,400]{0,1:T(8,128)}), f32[300,400]{0,1:T(8,128)}) %all-reduce.5.cloned.1.call-update) | async-done | bytes 480016 | tf_op jit(solution)/shard_map/psum | solution.py:83
  163.8 1.7 fusion.16
  165.5 1.8 fusion.32
  167.4 1.5 fusion.20
  169.0 1.8 fusion.36
  170.8 1.5 fusion.24
  174.5 7.4 %all_gather.3 = bf16[2,64,400]{2,1,0:T(8,128)(2,1)S(1)} all-gather(bf16[2,16,400]{2,1,0:T(8,128)(2,1)S(1)} %pad_maximum_fusion.1), channel_id=1, replica_groups=mesh['fluid'=8,'grp'=4] {'grp'}, dimensions={1}, use_global_device_ids=true | all-gather | bytes 128000 | tf_op jit(solution)/shard_map/all_gather | solution.py:106
  182.0 4.1 %fusion.4 = bf16[8192,128]{0,1:T(8,128)(2,1)S(1)} fusion(f32[128,8192]{1,0:T(8,128)S(1)} %copy-done.2, bf16[128,400]{1,0:T(8,128)(2,1)S(1)} %bitcast.38, bf16[8192,400]{0,1:T(8,128)(2,1)} %param.15), kind=kOutput, calls=%fused_computation.10 | convolution fusion | flops 840957952 | bytes 12947456 | tf_op jit(solution)/shard_map/dot_general | solution.py:108
  186.1 2.4 %copy.22 = bf16[8192,128]{1,0:T(8,128)(2,1)} copy(bf16[8192,128]{0,1:T(8,128)(2,1)S(1)} %fusion.4) | data formatting | bytes 4194304
  (68 shorter events, 7.4 us)
Async XLA Ops:
  7.2 80.4 %all-reduce.3.cloned.1.call-start = ((), (), s32[]{:S(2)}) async-start(), calls=%async_computation | async-start | bytes 1228800 | tf_op jit(solution)/shard_map/psum | solution.py:83
  7.9 10.7 %copy-start.6 = (s32[2048]{0:T(1024)S(1)}, s32[2048]{0:T(1024)}, u32[]{:S(2)}) copy-start(s32[2048]{0:T(1024)} %param.18) | copy-start | bytes 24580
  18.6 12.1 %copy-start.4 = (f32[2048]{0:T(1024)S(1)}, f32[2048]{0:T(1024)}, u32[]{:S(2)}) copy-start(f32[2048]{0:T(1024)} %param.20) | copy-start | bytes 24580
  36.7 18.5 %copy-start.11 = (f32[64]{0:T(128)S(1)}, f32[64]{0:T(128)}, u32[]{:S(2)}) copy-start(f32[64]{0:T(128)} %param.25) | copy-start | bytes 772
  36.7 18.5 %copy-start.7 = (f32[400]{0:T(512)S(1)}, f32[400]{0:T(512)}, u32[]{:S(2)}) copy-start(f32[400]{0:T(512)} %param.24) | copy-start | bytes 4804
  36.7 18.5 %copy-start.8 = (f32[400]{0:T(512)S(1)}, f32[400]{0:T(512)}, u32[]{:S(2)}) copy-start(f32[400]{0:T(512)} %param.23) | copy-start | bytes 4804
  36.7 18.5 %copy-start.5 = (f32[400]{0:T(512)S(1)}, f32[400]{0:T(512)}, u32[]{:S(2)}) copy-start(f32[400]{0:T(512)} %param.27) | copy-start | bytes 4804
  36.7 18.8 %copy-start.9 = (f32[300]{0:T(512)S(1)}, f32[300]{0:T(512)}, u32[]{:S(2)}) copy-start(f32[300]{0:T(512)} %param.22) | copy-start | bytes 3604
  36.8 18.8 %copy-start.10 = (f32[300]{0:T(512)S(1)}, f32[300]{0:T(512)}, u32[]{:S(2)}) copy-start(f32[300]{0:T(512)} %param.21) | copy-start | bytes 3604
  54.3 0.8 copy-start.1
  55.2 108.6 %all-reduce.5.cloned.1.call-start = ((), (), s32[]{:S(2)}) async-start(), calls=%async_computation.1 | async-start | bytes 1228800 | tf_op jit(solution)/shard_map/psum | solution.py:83
  87.5 77.9 %copy-start.3 = (f32[300]{0:T(512)S(1)}, f32[300]{0:T(512)}, u32[]{:S(2)}) copy-start(f32[300]{0:T(512)} %param.26) | copy-start | bytes 3604
  163.7 8.7 %copy-start = (f32[300,400]{0,1:T(8,128)S(1)}, f32[300,400]{0,1:T(8,128)}, u32[]{:S(2)}) copy-start(f32[300,400]{0,1:T(8,128)} %all-reduce.5.cloned.1.call-done) | copy-start | bytes 1440004
  163.7 18.2 %copy-start.2 = (f32[128,8192]{1,0:T(8,128)S(1)}, f32[128,8192]{1,0:T(8,128)}, u32[]{:S(2)}) copy-start(f32[128,8192]{1,0:T(8,128)} %fusion.12) | copy-start | bytes 12582916
Sparse Core Ops, SparseCore 0:
  55.3 32.1 all-reduce.2
  91.0 72.7 all-reduce.4
